TPU v7x, 512 devices: a whole 4x8x8 slice. The times are simulated.
512 devices in a mesh: depth: 64 (over x, y, core), samp: 8 (over z).
Axes of the slice: x: 4, y: 8, z: 8, core: 2. Of those that a mesh axis runs over, the one named last changes fastest.
Arguments:
- activations: bfloat16 [8, 64, 64, 16, 128], P('samp', 'depth'), may hold values from -6 to 6
- preact: bfloat16 [8, 64, 64, 16, 128], P('samp', 'depth'), may hold values from -6 to 6
- out_grad: bfloat16 [8, 64, 64, 16, 128], P('samp', 'depth'), may hold values from -6 to 6
- weights: bfloat16 [3, 3, 3, 128, 128], replicated, may hold values from -0.109375 to 0.109375
- master: float32 [442368], P(('depth', 'samp')), may hold values from -0.109375 to 0.109375
- moment: float32 [442368], P(('depth', 'samp')), may hold values from -4 to 4
- second: float32 [442368], P(('depth', 'samp')), may hold values from 0.1 to 1
Outputs:
- grad_input: bfloat16 [8, 64, 64, 16, 128], P('samp', 'depth')
- filter_grad: float32 [442368], P(('depth', 'samp'))
- new_moment: float32 [442368], P(('depth', 'samp'))
- new_second: float32 [442368], P(('depth', 'samp'))
- new_master: float32 [442368], P(('depth', 'samp'))
- new_weights: bfloat16 [3, 3, 3, 128, 128], replicated
All inputs are finite; a program needn't handle non-finite values.
Results may differ from a plain program's by a relative error of at most 0.001.
Values may be sent and summed in bfloat16 or wider, within the bound.
A program may use at most 64 MiB of HBM per device.

v0:
```python
import jax
import jax.numpy as jnp
from jax import lax
from jax.sharding import PartitionSpec as P

first_fix = 1.0
second_fix = 0.63230457524


def padded(array, sides, width):
    for axis, dim in sides:
        peers, length = (lax.axis_size(axis), array.shape[dim])
        up = [(i, (i + 1) % peers) for i in range(peers - 1)]
        down = [(j, i) for i, j in up]
        last = lax.slice_in_dim(array, length - width, length, axis=dim)
        first = lax.slice_in_dim(array, 0, width, axis=dim)
        before = lax.ppermute(last, axis, up)
        after = lax.ppermute(first, axis, down)
        array = jnp.concatenate([before, array, after], axis=dim)
    return array


def in_blocks(array, dim, peers):
    before, after = (array.shape[:dim], array.shape[dim + 1 :])
    return jnp.moveaxis(array.reshape(*before, peers, -1, *after), dim, 0)


def summed_on_arrival(array, axis, dim):
    peers = lax.axis_size(axis)
    tiles = lax.all_to_all(in_blocks(array, dim, peers), axis, 0, 0, tiled=True)
    return jnp.sum(tiles, axis=0)


def laid_out(tiles, dim):
    tiles = jnp.moveaxis(tiles, 0, dim)
    dims = tiles.shape
    return tiles.reshape(*dims[:dim], dims[dim] * dims[dim + 1], *dims[dim + 2 :])


def copy_for_each(array, axis):
    copies = jnp.broadcast_to(array, (lax.axis_size(axis), *array.shape))
    return lax.all_to_all(copies, axis, split_axis=0, concat_axis=0, tiled=True)


def gather_directly(array, axis, dim):
    return laid_out(copy_for_each(array, axis), dim)


def contract_rows(left, right):
    return lax.dot_general(
        left, right, (((0,), (0,)), ((), ())), preferred_element_type=jnp.float32
    )


def local(activations, preact, out_grad, weights, master, moment, second):
    samples = activations.shape[0]
    planes = activations.shape[1]
    height = activations.shape[2]
    width = activations.shape[3]
    chans = activations.shape[4]
    count = samples * lax.axis_size("samp") * planes * lax.axis_size("depth") * height * width
    slope = jnp.where(preact > 0, jnp.float32(1.0), jnp.float32(0.01))
    cotangent = (out_grad.astype(jnp.float32) * slope).astype(jnp.bfloat16)
    side_pad = ((0, 0), (0, 0), (1, 1), (1, 1), (0, 0))
    stacked = jnp.stack([activations, cotangent])
    extended = padded(stacked, (("depth", 2),), 1)
    padded_src = jnp.pad(extended[0], side_pad)
    padded_cot = jnp.pad(extended[1], side_pad)
    flat_cot = cotangent.reshape(-1, chans)
    result = jnp.zeros((samples * planes * height * width, chans), jnp.float32)
    terms = []
    for depth_tap in range(3):
        for row_tap in range(3):
            for col_tap in range(3):
                cot_part = padded_cot[
                    :,
                    2 - depth_tap : 2 - depth_tap + planes,
                    2 - row_tap : 2 - row_tap + height,
                    2 - col_tap : 2 - col_tap + width,
                ]
                cot_rows = cot_part.reshape(-1, chans)
                result = result + jnp.dot(
                    cot_rows,
                    weights[depth_tap, row_tap, col_tap].T,
                    preferred_element_type=jnp.float32,
                )
                src_part = padded_src[
                    :,
                    depth_tap : depth_tap + planes,
                    row_tap : row_tap + height,
                    col_tap : col_tap + width,
                ]
                terms.append(contract_rows(src_part.reshape(-1, chans), flat_cot))
    grad_input = result.reshape(samples, planes, height, width, chans).astype(jnp.bfloat16)
    local_grad = jnp.stack(terms).reshape(-1) * jnp.float32(1.0 / count**0.5)
    partial_value = summed_on_arrival(local_grad, "depth", 0)
    filter_grad = summed_on_arrival(partial_value, "samp", 0)
    new_moment = 0.9 * moment + 0.1 * filter_grad
    new_second = 0.999 * second + 0.001 * filter_grad * filter_grad
    new_master = master - 0.01 * (new_moment / first_fix) / (
        jnp.sqrt(new_second / second_fix) + 1e-08
    )
    share = new_master.astype(jnp.bfloat16)
    block = gather_directly(share, "samp", 0)
    whole = gather_directly(block, "depth", 0)
    new_weights = whole.reshape(3, 3, 3, chans, chans)
    return (grad_input, filter_grad, new_moment, new_second, new_master, new_weights)


def solution(mesh):
    return jax.shard_map(
        local,
        mesh=mesh,
        in_specs=(
            P("samp", "depth", None, None, None),
            P("samp", "depth", None, None, None),
            P("samp", "depth", None, None, None),
            P(),
            P(("depth", "samp")),
            P(("depth", "samp")),
            P(("depth", "samp")),
        ),
        out_specs=(
            P("samp", "depth", None, None, None),
            P(("depth", "samp")),
            P(("depth", "samp")),
            P(("depth", "samp")),
            P(("depth", "samp")),
            P(),
        ),
        check_vma=False,
    )
```

profile of v0, /device:TPU:1, one launch (start us, length us, event | category | flops | bytes accessed | tf_op | source)
XLA Modules:
  0.0 167.0 jit_solution(4457450354965144866)
XLA Ops:
  0.6 1.0 copy.175
  1.7 1.2 multiply_convert_fusion
  2.9 4.6 %collective-permute-start = (bf16[2,1,1,64,16,128]{5,3,4,2,1,0:T(8,128)(2,1)S(1)}, bf16[2,1,1,64,16,128]{5,3,4,2,1,0:T(8,128)(2,1)S(1)}, u32[]{:S(2)}, u32[]{:S(2)}) collective-permute-start(bf16[2,1,1,64,16,128]{5,3,4,2,1,0:T(8,128)(2,1)S(1)} %pad_maximum_fusion.1), channel_id=1, source_target_pairs={{0,8},{8,16},{16,24},{24,32},{32,40},{40,48},{48,56},{56,64},{64,7... | collective-permute-start | bytes 1572872 | tf_op jit(solution)/shard_map/ppermute | solution.py:17
  7.5 5.5 %collective-permute-start.1 = (bf16[2,1,1,64,16,128]{5,3,4,2,1,0:T(8,128)(2,1)S(1)}, bf16[2,1,1,64,16,128]{5,3,4,2,1,0:T(8,128)(2,1)S(1)}, u32[]{:S(2)}, u32[]{:S(2)}) collective-permute-start(bf16[2,1,1,64,16,128]{5,3,4,2,1,0:T(8,128)(2,1)S(1)} %pad_maximum_fusion.1), channel_id=1, source_target_pairs={{8,0},{16,8},{24,16},{32,24},{40,32},{48,40},{56,48},{64,56},{72,6... | collective-permute-start | bytes 1572872 | tf_op jit(solution)/shard_map/ppermute | solution.py:18
  13.0 0.6 collective-permute-done
  13.6 4.4 %collective-permute-done.1 = bf16[2,1,1,64,16,128]{5,3,4,2,1,0:T(8,128)(2,1)S(1)} collective-permute-done((bf16[2,1,1,64,16,128]{5,3,4,2,1,0:T(8,128)(2,1)S(1)}, bf16[2,1,1,64,16,128]{5,3,4,2,1,0:T(8,128)(2,1)S(1)}, u32[]{:S(2)}, u32[]{:S(2)}) %collective-permute-start.1) | collective-permute-done | bytes 524320 | tf_op jit(solution)/shard_map/ppermute | solution.py:18
  18.3 2.8 %pad_slice_fusion.24 = (bf16[1,1,64,16,128]{4,2,3,1,0:T(8,128)(2,1)}, bf16[1,1,64,16,128]{4,2,3,1,0:T(8,128)(2,1)}, bf16[1,1,64,16,128]{4,2,3,1,0:T(8,128)(2,1)}...) fusion(bf16[1,3,64,16,128]{4,2,3,1,0:T(8,128)(2,1)S(1)} %get-tu, ...), kind=kLoop, calls=%fused_computation.109 | loop fusion | bytes 5767168 | tf_op jit(solution)/shard_map/slice | solution.py:75
  21.1 1.1 pad_slice_fusion.25
  22.2 0.3 fusion.27
  22.5 0.3 fusion.26
  22.8 0.3 fusion.25
  23.9 0.3 fusion.21
  24.1 0.3 fusion.20
  24.4 0.3 fusion.19
  24.7 0.3 fusion.18
  25.0 0.3 fusion.17
  25.2 0.3 fusion.16
  26.3 0.3 fusion.12
  26.6 0.3 fusion.11
  26.9 0.3 fusion.10
  27.2 0.3 fusion.9
  27.4 0.3 fusion.8
  27.7 0.3 fusion.7
  28.8 0.3 fusion.3
  29.1 0.3 fusion.2
  29.4 0.3 fusion.1
  29.6 1.4 broadcast_multiply_fusion
  31.1 10.4 %all-to-all-start = ((f32[64,1,6912]{2,1,0:T(1,128)}), f32[64,1,6912]{2,1,0:T(1,128)S(1)}, u32[]{:S(2)}, u32[]{:S(2)}) async-start(f32[64,1,6912]{2,1,0:T(1,128)} %bitcast.141), calls=%async_computation | async-start | bytes 3538944 | tf_op jit(solution)/shard_map/all_to_all | solution.py:30
  41.5 1.2 copy.143
  42.9 1.1 copy.144
  44.0 1.1 copy.145
  52.7 32.8 %all-to-all-done = f32[64,1,6912]{2,1,0:T(1,128)S(1)} async-done(((f32[64,1,6912]{2,1,0:T(1,128)}), f32[64,1,6912]{2,1,0:T(1,128)S(1)}, u32[]{:S(2)}, u32[]{:S(2)}) %all-to-all-start) | async-done | bytes 1769504 | tf_op jit(solution)/shard_map/all_to_all | solution.py:30
  85.5 1.0 reduce_sum.18
  86.5 0.7 all_to_all.19
  87.3 10.0 %all-to-all-start.1 = ((f32[8,1,864]{2,1,0:T(1,128)}), f32[8,1,864]{2,1,0:T(1,128)S(1)}, u32[]{:S(2)}, u32[]{:S(2)}) async-start(f32[8,1,864]{2,1,0:T(1,128)} %all_to_all.19), calls=%async_computation.1 | async-start | bytes 57344 | tf_op jit(solution)/shard_map/all_to_all | solution.py:30
  97.3 1.0 convolution_add_fusion.8
  98.5 5.6 %all-to-all-done.1 = f32[8,1,864]{2,1,0:T(1,128)S(1)} async-done(((f32[8,1,864]{2,1,0:T(1,128)}), f32[8,1,864]{2,1,0:T(1,128)S(1)}, u32[]{:S(2)}, u32[]{:S(2)}) %all-to-all-start.1) | async-done | bytes 27680 | tf_op jit(solution)/shard_map/all_to_all | solution.py:30
  104.2 0.6 fusion.183
  104.8 0.6 broadcast.23
  105.4 0.8 reduce.4
  106.2 0.7 reshape.364
  106.9 3.5 %all-to-all-start.2 = ((bf16[8,2,432]{2,1,0:T(2,128)(2,1)}), bf16[8,2,432]{2,1,0:T(2,128)(2,1)S(1)}, u32[]{:S(2)}, u32[]{:S(2)}) async-start(bf16[8,2,432]{2,1,0:T(2,128)(2,1)} %reshape.364), calls=%async_computation.2 | async-start | bytes 32768 | tf_op jit(solution)/shard_map/all_to_all | solution.py:42
  110.4 1.0 convolution_add_fusion.7
  111.4 1.9 %copy.162 = bf16[1,1,64,16,128]{4,3,2,1,0:T(8,128)(2,1)} copy(bf16[1,1,64,16,128]{4,2,3,1,0:T(8,128)(2,1)} %get-tuple-element.30) | data formatting | bytes 524288 | tf_op jit(solution)/shard_map/slice | solution.py:75
  113.3 0.9 copy.163
  114.2 0.9 copy.164
  115.1 0.9 copy.165
  115.9 0.9 copy.166
  117.0 0.9 copy.168
  118.2 0.9 broadcast_in_dim.20
  119.1 6.0 %reduce.5 = bf16[64,6912]{1,0:T(8,128)(2,1)S(1)} reduce(bf16[64,1,6912]{2,1,0:T(2,128)(2,1)S(1)} %broadcast_in_dim.20, bf16[]{:T(256)} %broadcast.23), dimensions={1}, to_apply=%broadcast_in_dim.20.reduce_sub_computation | reduce | bytes 1769474 | tf_op jit(solution)/shard_map/broadcast_in_dim | solution.py:41
  125.1 1.1 reshape.366
  126.2 7.6 %all-to-all-start.3 = ((bf16[64,2,3456]{2,1,0:T(2,128)(2,1)}), bf16[64,2,3456]{2,1,0:T(2,128)(2,1)S(1)}, u32[]{:S(2)}, u32[]{:S(2)}) async-start(bf16[64,2,3456]{2,1,0:T(2,128)(2,1)} %reshape.366), calls=%async_computation.3 | async-start | bytes 1769472 | tf_op jit(solution)/shard_map/all_to_all | solution.py:42
  133.9 1.0 convolution_add_fusion.6
  134.9 1.0 convolution_add_fusion.5
  136.0 1.0 convolution_add_fusion.4
  137.0 1.0 convolution_add_fusion.3
  138.1 1.0 convolution_add_fusion.2
  139.0 1.0 convolution_add_fusion.1
  140.0 1.7 %fusion = bf16[1024,128]{1,0:T(8,128)(2,1)} fusion(f32[1024,128]{1,0:T(8,128)S(1)} %convolution_add_fusion.1, bf16[1024,128]{1,0:T(8,128)(2,1)S(1)} %bitcast.424, bf16[3,3,3,128,128]{4,3,2,1,0:T(8,128)(2,1)} %param.10), kind=kOutput, calls=%fused_computation.27 | convolution fusion | flops 33816576 | bytes 1081344 | tf_op jit(solution)/shard_map/dot_general | solution.py:82
  141.7 17.1 %all-to-all-done.3 = bf16[64,2,3456]{2,1,0:T(2,128)(2,1)S(1)} async-done(((bf16[64,2,3456]{2,1,0:T(2,128)(2,1)}), bf16[64,2,3456]{2,1,0:T(2,128)(2,1)S(1)}, u32[]{:S(2)}, u32[]{:S(2)}) %all-to-all-start.3) | async-done | bytes 884768 | tf_op jit(solution)/shard_map/all_to_all | solution.py:42
  158.9 0.7 reshape.367
  159.6 5.3 %reduce.3 = bf16[64,6912]{1,0:T(8,128)(2,1)S(1)} reduce(bf16[64,1,6912]{2,1,0:T(2,128)(2,1)S(1)} %reshape.367, bf16[]{:T(256)} %constant.37), dimensions={1}, to_apply=%all_to_all.22.reduce_sub_computation | reduce | bytes 1769474 | tf_op jit(solution)/shard_map/all_to_all | solution.py:42
  164.9 2.1 %reshape_reshape.3 = bf16[3,3,3,128,128]{4,3,2,1,0:T(8,128)(2,1)} reshape(bf16[64,6912]{1,0:T(8,128)(2,1)S(1)} %reduce.3) | data formatting | bytes 1769472 | tf_op jit(solution)/shard_map/reshape;reshape | solution.py:106
  (110 shorter events, 10.7 us)
Async XLA Ops:
  2.9 10.7 %collective-permute-start = (bf16[2,1,1,64,16,128]{5,3,4,2,1,0:T(8,128)(2,1)S(1)}, bf16[2,1,1,64,16,128]{5,3,4,2,1,0:T(8,128)(2,1)S(1)}, u32[]{:S(2)}, u32[]{:S(2)}) collective-permute-start(bf16[2,1,1,64,16,128]{5,3,4,2,1,0:T(8,128)(2,1)S(1)} %pad_maximum_fusion.1), channel_id=1, source_target_pairs={{0,8},{8,16},{16,24},{24,32},{32,40},{40,48},{48,56},{56,64},{64,7... | collective-permute-start | bytes 1572872 | tf_op jit(solution)/shard_map/ppermute | solution.py:17
  7.5 10.5 %collective-permute-start.1 = (bf16[2,1,1,64,16,128]{5,3,4,2,1,0:T(8,128)(2,1)S(1)}, bf16[2,1,1,64,16,128]{5,3,4,2,1,0:T(8,128)(2,1)S(1)}, u32[]{:S(2)}, u32[]{:S(2)}) collective-permute-start(bf16[2,1,1,64,16,128]{5,3,4,2,1,0:T(8,128)(2,1)S(1)} %pad_maximum_fusion.1), channel_id=1, source_target_pairs={{8,0},{16,8},{24,16},{32,24},{40,32},{48,40},{56,48},{64,56},{72,6... | collective-permute-start | bytes 1572872 | tf_op jit(solution)/shard_map/ppermute | solution.py:18
  31.1 54.4 %all-to-all-start = ((f32[64,1,6912]{2,1,0:T(1,128)}), f32[64,1,6912]{2,1,0:T(1,128)S(1)}, u32[]{:S(2)}, u32[]{:S(2)}) async-start(f32[64,1,6912]{2,1,0:T(1,128)} %bitcast.141), calls=%async_computation | async-start | bytes 3538944 | tf_op jit(solution)/shard_map/all_to_all | solution.py:30
  41.5 3.8 %copy-start.23 = (bf16[3,3,3,128,128]{4,3,2,1,0:T(8,128)(2,1)S(1)}, bf16[3,3,3,128,128]{4,3,2,1,0:T(8,128)(2,1)}, u32[]{:S(2)}) copy-start(bf16[3,3,3,128,128]{4,3,2,1,0:T(8,128)(2,1)} %param.10) | copy-start | bytes 2654212
  45.8 1.0 copy-start.16
  46.1 1.0 copy-start.15
  46.1 1.1 copy-start.14
  46.3 1.1 copy-start.13
  46.3 1.3 copy-start.12
  46.4 1.5 copy-start.11
  46.6 1.4 copy-start.10
  46.8 1.5 copy-start.9
  47.2 1.4 copy-start.8
  47.4 1.4 copy-start.7
  47.6 1.4 copy-start.6
  47.8 1.3 copy-start.5
  48.0 1.3 copy-start.4
  52.6 51.5 %copy-start.25 = (f32[864]{0:T(1024)S(1)}, f32[864]{0:T(1024)}, u32[]{:S(2)}) copy-start(f32[864]{0:T(1024)} %param.11) | copy-start | bytes 10372
  52.7 51.5 %copy-start.26 = (f32[864]{0:T(1024)S(1)}, f32[864]{0:T(1024)}, u32[]{:S(2)}) copy-start(f32[864]{0:T(1024)} %param.13) | copy-start | bytes 10372
  52.7 51.5 %copy-start.27 = (f32[864]{0:T(1024)S(1)}, f32[864]{0:T(1024)}, u32[]{:S(2)}) copy-start(f32[864]{0:T(1024)} %param.12) | copy-start | bytes 10372
  87.3 16.9 %all-to-all-start.1 = ((f32[8,1,864]{2,1,0:T(1,128)}), f32[8,1,864]{2,1,0:T(1,128)S(1)}, u32[]{:S(2)}, u32[]{:S(2)}) async-start(f32[8,1,864]{2,1,0:T(1,128)} %all_to_all.19), calls=%async_computation.1 | async-start | bytes 57344 | tf_op jit(solution)/shard_map/all_to_all | solution.py:30
  97.3 16.0 %copy-start.2 = (bf16[1,1,64,16,128]{4,2,3,1,0:T(8,128)(2,1)S(1)}, bf16[1,1,64,16,128]{4,2,3,1,0:T(8,128)(2,1)}, u32[]{:S(2)}) copy-start(bf16[1,1,64,16,128]{4,2,3,1,0:T(8,128)(2,1)} %get-tuple-element.32) | copy-start | bytes 786436
  98.3 15.8 %copy-start.1 = (bf16[1,1,64,16,128]{4,2,3,1,0:T(8,128)(2,1)S(1)}, bf16[1,1,64,16,128]{4,2,3,1,0:T(8,128)(2,1)}, u32[]{:S(2)}) copy-start(bf16[1,1,64,16,128]{4,2,3,1,0:T(8,128)(2,1)} %get-tuple-element.35) | copy-start | bytes 786436
  98.3 16.7 %copy-start = (bf16[1,1,64,16,128]{4,2,3,1,0:T(8,128)(2,1)S(1)}, bf16[1,1,64,16,128]{4,2,3,1,0:T(8,128)(2,1)}, u32[]{:S(2)}) copy-start(bf16[1,1,64,16,128]{4,2,3,1,0:T(8,128)(2,1)} %get-tuple-element.33) | copy-start | bytes 786436
  104.2 11.8 %copy-start.24 = (f32[864]{0:T(1024)}, f32[864]{0:T(1024)S(1)}, u32[]{:S(2)}) copy-start(f32[864]{0:T(1024)S(1)} %reduce_sum.19) | copy-start | bytes 10372
  106.9 11.0 %all-to-all-start.2 = ((bf16[8,2,432]{2,1,0:T(2,128)(2,1)}), bf16[8,2,432]{2,1,0:T(2,128)(2,1)S(1)}, u32[]{:S(2)}, u32[]{:S(2)}) async-start(bf16[8,2,432]{2,1,0:T(2,128)(2,1)} %reshape.364), calls=%async_computation.2 | async-start | bytes 32768 | tf_op jit(solution)/shard_map/all_to_all | solution.py:42
  111.4 5.6 %copy-start.3 = (bf16[1,1,64,16,128]{4,2,3,1,0:T(8,128)(2,1)S(1)}, bf16[1,1,64,16,128]{4,2,3,1,0:T(8,128)(2,1)}, u32[]{:S(2)}) copy-start(bf16[1,1,64,16,128]{4,2,3,1,0:T(8,128)(2,1)} %get-tuple-element.12) | copy-start | bytes 786436
  125.1 8.8 %copy-start.21 = (bf16[1,1,64,16,128]{4,3,2,1,0:T(8,128)(2,1)S(1)}, bf16[1,1,64,16,128]{4,3,2,1,0:T(8,128)(2,1)}, u32[]{:S(2)}) copy-start(bf16[1,1,64,16,128]{4,3,2,1,0:T(8,128)(2,1)} %copy.162) | copy-start | bytes 786436
  126.2 8.7 %copy-start.22 = (bf16[1,1,64,16,128]{4,3,2,1,0:T(8,128)(2,1)S(1)}, bf16[1,1,64,16,128]{4,3,2,1,0:T(8,128)(2,1)}, u32[]{:S(2)}) copy-start(bf16[1,1,64,16,128]{4,3,2,1,0:T(8,128)(2,1)} %copy.163) | copy-start | bytes 786436
  126.2 32.6 %all-to-all-start.3 = ((bf16[64,2,3456]{2,1,0:T(2,128)(2,1)}), bf16[64,2,3456]{2,1,0:T(2,128)(2,1)S(1)}, u32[]{:S(2)}, u32[]{:S(2)}) async-start(bf16[64,2,3456]{2,1,0:T(2,128)(2,1)} %reshape.366), calls=%async_computation.3 | async-start | bytes 1769472 | tf_op jit(solution)/shard_map/all_to_all | solution.py:42
  133.9 2.1 %copy-start.20 = (bf16[1,1,64,16,128]{4,3,2,1,0:T(8,128)(2,1)S(1)}, bf16[1,1,64,16,128]{4,3,2,1,0:T(8,128)(2,1)}, u32[]{:S(2)}) copy-start(bf16[1,1,64,16,128]{4,3,2,1,0:T(8,128)(2,1)} %copy.164) | copy-start | bytes 786436
  133.9 3.1 %copy-start.19 = (bf16[1,1,64,16,128]{4,3,2,1,0:T(8,128)(2,1)S(1)}, bf16[1,1,64,16,128]{4,3,2,1,0:T(8,128)(2,1)}, u32[]{:S(2)}) copy-start(bf16[1,1,64,16,128]{4,3,2,1,0:T(8,128)(2,1)} %copy.165) | copy-start | bytes 786436
  134.9 3.1 %copy-start.17 = (bf16[1,1,64,16,128]{4,3,2,1,0:T(8,128)(2,1)S(1)}, bf16[1,1,64,16,128]{4,3,2,1,0:T(8,128)(2,1)}, u32[]{:S(2)}) copy-start(bf16[1,1,64,16,128]{4,3,2,1,0:T(8,128)(2,1)} %copy.166) | copy-start | bytes 786436
  137.0 3.0 %copy-start.18 = (bf16[1,1,64,16,128]{4,3,2,1,0:T(8,128)(2,1)S(1)}, bf16[1,1,64,16,128]{4,3,2,1,0:T(8,128)(2,1)}, u32[]{:S(2)}) copy-start(bf16[1,1,64,16,128]{4,3,2,1,0:T(8,128)(2,1)} %copy.168) | copy-start | bytes 786436
where the time goes:
time: 168 us; the launch traced here: 167 us
  waiting for transfers between devices  60.5 us (36%)
  starting transfers between devices  41.7 us (25%)
  local copies, waits for them, and re-layouts  25.4 us (15%)
  matrix products  21.1 us (13%)
  other arithmetic  16.7 us (10%)
    all_to_all x2, waiting for transfers between devices, summed_on_arrival(): tiles = lax.all_to_all(in_blocks(array, dim, peers), axis, 0, 0, tiled=True)  38.4 us
    all_to_all x2, starting transfers between devices, summed_on_arrival(): tiles = lax.all_to_all(in_blocks(array, dim, peers), axis, 0, 0, tiled=True)  20.5 us
    all_to_all x2, waiting for transfers between devices, copy_for_each(): return lax.all_to_all(copies, axis, split_axis=0, concat_axis=0, tiled=True)  17.1 us
    slice x29, local copies, waits for them, and re-layouts, local(): padded_cot[:, 2 - depth_tap:2 - depth_tap + planes, 2 - row_tap:2 - row_t...  16.8 us
    dot_general x27, matrix products, local(): jnp.dot(cot_rows, weights[depth_tap, row_tap, col_tap].T, preferred_eleme...  13.9 us
    all_to_all x2, starting transfers between devices, copy_for_each(): return lax.all_to_all(copies, axis, split_axis=0, concat_axis=0, tiled=True)  11.1 us
    dot_general x27, matrix products, contract_rows(): lax.dot_general(left, right, (((0,), (0,)), ((), ())), preferred_element_...  7.22 us
    broadcast_in_dim x2, other arithmetic, copy_for_each(): copies = jnp.broadcast_to(array, (lax.axis_size(axis), *array.shape))  6.75 us
  transfers between devices with their start and end apart: 6, of which 5 were waited for; matrix products, arithmetic and copies ran while one was open for 16% of the time, Pallas kernels for 0%

commit v1 on v0

v1 whole, which is shorter than its diff:
```python
import jax
import jax.numpy as jnp
from jax import lax
from jax.experimental import pallas as pl
from jax.experimental.pallas import tpu as pltpu
from jax.sharding import PartitionSpec as P

first_fix = 1.0
second_fix = 0.63230457524

NX, NY, NC, NZ = 4, 8, 2, 8
H, W, CH = 64, 16, 128
POS = H * W
ROWS = 54
PAD = 56
SHARE = 864
COUNT = 8 * 64 * H * W
MESH = pl.DeviceIdType.MESH


def first_row(z):
    return (27 * z) // 4


def kernel(
    act_hbm, pre_hbm, og_hbm, w_hbm, opt_ref,
    gi_ref, fg_ref, nm_ref, ns_ref, nma_ref, nw_ref,
    act, pre, og, wts, in_sem,
    cc, halo, halo_s, halo_r,
    xs, act_t, flat, grid,
    r0, r0_s, r0_r,
    s1, r1, r1_s, r1_r,
    s2, r2, r2_s, r2_r,
    s3, win, r3, r3_s, r3_r,
    out_win, r4, r4_s, r4_r, block,
    full, y_s, y_r, x_s, x_r, c_s, c_r,
):
    p = lax.axis_index("depth")
    z = lax.axis_index("samp")
    n_depth = NX * NY * NC
    c = lax.rem(p, NC)
    y = lax.rem(p // NC, NY)
    x = p // (NC * NY)

    def dev(xx, yy, ccore, zz):
        return {"depth": (xx * NY + yy) * NC + ccore, "samp": zz}

    below = {"depth": lax.rem(p + n_depth - 1, n_depth), "samp": z}
    above = {"depth": lax.rem(p + 1, n_depth), "samp": z}
    partner = dev(x, y, 1 - c, z)
    x_peer = [dev(lax.rem(x + k, NX), y, c, z) for k in range(NX)]
    y_peer = [dev(x, lax.rem(y + k, NY), c, z) for k in range(NY)]
    z_peer = [dev(x, y, c, lax.rem(z + k, NZ)) for k in range(NZ)]

    barrier = pltpu.get_barrier_semaphore()
    peers = [below, above] + x_peer[1:] + y_peer[1:] + z_peer[1:]
    for peer in peers:
        pl.semaphore_signal(barrier, inc=1, device_id=peer, device_id_type=MESH)

    loads = [
        pltpu.make_async_copy(src, dst, in_sem.at[i])
        for i, (src, dst) in enumerate(
            ((pre_hbm, pre), (og_hbm, og), (act_hbm, act), (w_hbm, wts))
        )
    ]
    for load in loads:
        load.start()
    loads[0].wait()
    loads[1].wait()

    @pl.loop(0, 8)
    def _(i):
        part = pl.ds(i * 8, 8)
        slope = jnp.where(pre[part].astype(jnp.float32) > 0, jnp.float32(1.0), jnp.float32(0.01))
        cc[part] = (og[part].astype(jnp.float32) * slope).astype(jnp.bfloat16)

    pl.semaphore_wait(barrier, len(peers))

    def remote(src, dst, s, r, to):
        return pltpu.make_async_remote_copy(
            src_ref=src, dst_ref=dst, send_sem=s, recv_sem=r, device_id=to, device_id_type=MESH
        )

    halo_copies = [
        remote(cc, halo.at[0], halo_s.at[0], halo_r.at[0], above),
        remote(cc, halo.at[1], halo_s.at[1], halo_r.at[1], below),
    ]
    for copy in halo_copies:
        copy.start()

    def spread(src, plane, keep):
        zero_row = jnp.zeros((W, CH), jnp.bfloat16)
        for col in range(3):
            xs[col, plane, 0] = zero_row
            xs[col, plane, H + 1] = zero_row

        @pl.loop(0, 8)
        def _(i):
            v = src[pl.ds(i * 8, 8)].astype(jnp.float32).reshape(8 * W, CH)
            if keep is not None:
                v = jnp.where(keep, v, 0.0)
            w = lax.broadcasted_iota(jnp.int32, (8 * W, CH), 0) % W
            after = jnp.where(w == W - 1, 0.0, pltpu.roll(v, 8 * W - 1, 0))
            before = jnp.where(w == 0, 0.0, pltpu.roll(v, 1, 0))
            for col, moved in ((0, after), (1, v), (2, before)):
                xs[col, plane, pl.ds(1 + i * 8, 8)] = moved.reshape(8, W, CH).astype(jnp.bfloat16)

    def taps(a):
        @pl.loop(0, 3)
        def _(b):
            right = jnp.concatenate(
                [xs[col, 2 - a, pl.ds(2 - b, H)].reshape(POS, CH) for col in range(3)], axis=1
            )
            raw = jnp.dot(act_t[...], right, preferred_element_type=jnp.float32)
            for col in range(3):
                row = pl.multiple_of(((a * 3 + b) * 3 + col) * CH, CH)
                flat[pl.ds(row, CH)] = raw[:, col * CH : (col + 1) * CH]

    loads[2].wait()
    act_t[...] = act[...].reshape(POS, CH).astype(jnp.float32).T.astype(jnp.bfloat16)
    spread(cc, 1, None)
    taps(1)
    halo_copies[0].wait_recv()
    spread(halo.at[0], 0, p > 0)
    taps(2)
    halo_copies[1].wait_recv()
    spread(halo.at[1], 2, p < n_depth - 1)
    taps(0)

    core_copies = []
    for xx in range(NX):

        @pl.loop(0, NY)
        def _(yy):
            for cr in range(NC):
                start = ((xx * NY + yy) * NC + cr) * ROWS
                grid[cr, xx, yy, 0:ROWS] = flat[pl.ds(start, ROWS)]

        copy = remote(grid.at[1 - c, xx], r0.at[xx], r0_s.at[xx], r0_r.at[xx], partner)
        copy.start()
        core_copies.append(copy)
    for xx in range(NX):
        core_copies[xx].wait_recv()

        @pl.loop(0, NY)
        def _(yy):
            s1[xx, yy] = grid[c, xx, yy] + r0[xx, yy]

    x_copies = []
    for k in (2, 1, 3):
        copy = remote(
            s1.at[lax.rem(x + k, NX)], r1.at[k - 1], r1_s.at[k - 1], r1_r.at[k - 1], x_peer[k]
        )
        copy.start()
        x_copies.append(copy)

    loads[3].wait()

    @pl.loop(0, 4)
    def _(m):
        acc = jnp.zeros((POS // 4, CH), jnp.float32)
        for a in range(3):
            for b in range(3):
                left = jnp.concatenate(
                    [
                        xs[col, 2 - a, pl.ds(2 - b + m * (H // 4), H // 4)].reshape(POS // 4, CH)
                        for col in range(3)
                    ],
                    axis=1,
                )
                right = jnp.concatenate([wts[(a * 3 + b) * 3 + col] for col in range(3)], axis=1)
                acc = acc + lax.dot_general(
                    left, right, (((1,), (1,)), ((), ())), preferred_element_type=jnp.float32
                )
        gi_ref[pl.ds(m * (H // 4), H // 4)] = acc.reshape(H // 4, W, CH).astype(jnp.bfloat16)

    for copy in x_copies:
        copy.wait_recv()

    @pl.loop(0, NY)
    def _(yy):
        s2[yy] = s1[x, yy] + r1[0, yy] + r1[1, yy] + r1[2, yy]

    y_copies = []
    for k in (4, 3, 5, 2, 6, 1, 7):
        copy = remote(
            s2.at[lax.rem(y + k, NY)], r2.at[k - 1], r2_s.at[k - 1], r2_r.at[k - 1], y_peer[k]
        )
        copy.start()
        y_copies.append(copy)
    for copy in y_copies:
        copy.wait_recv()
    total = s2[y]
    for k in range(1, NY):
        total = total + r2[k - 1]
    s3[...] = total

    for zz in range(NZ):
        win[zz] = s3[first_row(zz) : first_row(zz) + 8]
    z_copies = []
    for k in (4, 3, 5, 2, 6, 1, 7):
        copy = remote(
            win.at[lax.rem(z + k, NZ)], r3.at[k - 1], r3_s.at[k - 1], r3_r.at[k - 1], z_peer[k]
        )
        copy.start()
        z_copies.append(copy)
    for copy in z_copies:
        copy.wait_recv()
    raw = win[z]
    for k in range(1, NZ):
        raw = raw + r3[k - 1]

    off = lax.rem(96 * z, 128)
    lane = lax.broadcasted_iota(jnp.int32, (8, CH), 1)
    row = lax.broadcasted_iota(jnp.int32, (8, CH), 0)
    turned = pltpu.roll(raw, lax.rem(128 - off, 128), 1)
    raw = jnp.where(lane < 128 - off, turned, pltpu.roll(turned, 7, 0))
    filter_grad = raw * jnp.float32(1.0 / COUNT**0.5)
    new_moment = 0.9 * opt_ref[1] + 0.1 * filter_grad
    new_second = 0.999 * opt_ref[2] + 0.001 * filter_grad * filter_grad
    new_master = opt_ref[0] - 0.01 * (new_moment / first_fix) / (
        jnp.sqrt(new_second / second_fix) + 1e-08
    )
    fg_ref[...] = filter_grad
    nm_ref[...] = new_moment
    ns_ref[...] = new_second
    nma_ref[...] = new_master

    turned = pltpu.roll(new_master, off, 1)
    moved = jnp.where(lane >= off, turned, pltpu.roll(turned, 1, 0))
    place = row * CH + lane
    mine = jnp.where((place >= off) & (place < off + SHARE), moved, 0.0)
    out_win[...] = mine
    r4[z] = mine
    share_copies = []
    for k in (4, 3, 5, 2, 6, 1, 7):
        copy = remote(out_win, r4.at[z], r4_s.at[k - 1], r4_r.at[k - 1], z_peer[k])
        copy.start()
        share_copies.append(copy)
    for copy in share_copies:
        copy.wait_recv()
    block[...] = jnp.zeros_like(block)
    for zz in range(NZ):
        part = pl.ds(first_row(zz), 8)
        block[part] = block[part] + r4[zz]
    full[c, x, y] = block[0:PAD].astype(jnp.bfloat16)

    gather_y = []
    for k in (4, 3, 5, 2, 6, 1, 7):
        copy = remote(
            full.at[c, x, y], full.at[c, x, y], y_s.at[k - 1], y_r.at[k - 1], y_peer[k]
        )
        copy.start()
        gather_y.append(copy)
    for copy in gather_y:
        copy.wait_recv()

    gather_x = {}
    for k in (2, 1, 3):
        gather_x[k] = remote(full.at[c, x], full.at[c, x], x_s.at[k - 1], x_r.at[k - 1], x_peer[k])
        gather_x[k].start()
    gather_c = []
    for k in (0, 1, 3, 2):
        if k:
            gather_x[k].wait_recv()
        came = lax.rem(x + NX - k, NX)
        copy = remote(full.at[c, came], full.at[c, came], c_s.at[k], c_r.at[k], partner)
        copy.start()
        gather_c.append(copy)
    for copy in gather_c:
        copy.wait_recv()
    for xx in range(NX):
        for yy in range(NY):
            for cr in range(NC):
                start = ((xx * NY + yy) * NC + cr) * ROWS
                nw_ref[start : start + ROWS] = full[cr, xx, yy, 0:ROWS]

    sends = halo_copies + core_copies + x_copies + y_copies + z_copies + share_copies
    for copy in sends + gather_y + list(gather_x.values()) + gather_c:
        copy.wait_send()


def step(activations, preact, out_grad, weights, opt):
    vmem = pl.BlockSpec(memory_space=pltpu.VMEM)
    hbm = pl.BlockSpec(memory_space=pl.ANY)
    f32, bf16 = jnp.float32, jnp.bfloat16
    dma = pltpu.SemaphoreType.DMA
    shape = jax.ShapeDtypeStruct
    return pl.pallas_call(
        kernel,
        out_shape=(
            shape((H, W, CH), bf16),
            shape((8, CH), f32),
            shape((8, CH), f32),
            shape((8, CH), f32),
            shape((8, CH), f32),
            shape((NX * NY * NC * ROWS, CH), bf16),
        ),
        in_specs=[hbm, hbm, hbm, hbm, vmem],
        out_specs=(vmem,) * 6,
        scratch_shapes=[
            pltpu.VMEM((H, W, CH), bf16),
            pltpu.VMEM((H, W, CH), bf16),
            pltpu.VMEM((H, W, CH), bf16),
            pltpu.VMEM((27, CH, CH), bf16),
            dma((4,)),
            pltpu.VMEM((H, W, CH), bf16),
            pltpu.VMEM((2, H, W, CH), bf16),
            dma((2,)),
            dma((2,)),
            pltpu.VMEM((3, 3, H + 2, W, CH), bf16),
            pltpu.VMEM((CH, POS), bf16),
            pltpu.VMEM((NX * NY * NC * ROWS, CH), f32),
            pltpu.VMEM((NC, NX, NY, PAD, CH), f32),
            pltpu.VMEM((NX, NY, PAD, CH), f32),
            dma((NX,)),
            dma((NX,)),
            pltpu.VMEM((NX, NY, PAD, CH), f32),
            pltpu.VMEM((NX - 1, NY, PAD, CH), f32),
            dma((NX - 1,)),
            dma((NX - 1,)),
            pltpu.VMEM((NY, PAD, CH), f32),
            pltpu.VMEM((NY - 1, PAD, CH), f32),
            dma((NY - 1,)),
            dma((NY - 1,)),
            pltpu.VMEM((PAD, CH), f32),
            pltpu.VMEM((NZ, 8, CH), f32),
            pltpu.VMEM((NZ - 1, 8, CH), f32),
            dma((NZ - 1,)),
            dma((NZ - 1,)),
            pltpu.VMEM((8, CH), f32),
            pltpu.VMEM((NZ, 8, CH), f32),
            dma((NZ - 1,)),
            dma((NZ - 1,)),
            pltpu.VMEM((64, CH), f32),
            pltpu.VMEM((NC, NX, NY, PAD, CH), bf16),
            dma((NY - 1,)),
            dma((NY - 1,)),
            dma((NX - 1,)),
            dma((NX - 1,)),
            dma((NX,)),
            dma((NX,)),
        ],
        compiler_params=pltpu.CompilerParams(
            collective_id=0, has_side_effects=True, vmem_limit_bytes=40 * 1024 * 1024
        ),
        name="conv_step",
    )(activations, preact, out_grad, weights, opt)


def local(activations, preact, out_grad, weights, master, moment, second):
    plane = (H, W, CH)
    opt = jnp.pad(jnp.stack([master, moment, second]), ((0, 0), (0, 8 * CH - SHARE)))
    gi, fg, nm, ns, nma, nw = step(
        activations.reshape(plane),
        preact.reshape(plane),
        out_grad.reshape(plane),
        weights.reshape(27, CH, CH),
        opt.reshape(3, 8, CH),
    )
    own = [a.reshape(-1)[:SHARE] for a in (fg, nm, ns, nma)]
    return (gi.reshape(activations.shape), *own, nw.reshape(weights.shape))


def solution(mesh):
    volume = P("samp", "depth", None, None, None)
    shares = P(("depth", "samp"))
    return jax.shard_map(
        local,
        mesh=mesh,
        in_specs=(volume, volume, volume, P(), shares, shares, shares),
        out_specs=(volume, shares, shares, shares, shares, P()),
        check_vma=False,
    )
```

time: 168 us -> 76.1 us (0.45)
  Pallas kernels: 0 us -> 65 us
  waiting for transfers between devices: 60.5 us -> 0 us
  starting transfers between devices: 41.7 us -> 0 us
  matrix products: 21.1 us -> 0 us
  other arithmetic: 16.7 us -> 0.02 us
  local copies, waits for them, and re-layouts: 25.4 us -> 10.1 us
    pallas_call x0 -> x1, Pallas kernels: none -> 65 us  [step(): pl.pallas_call(kernel, out_shape=(shape((H, W, CH), bf16), shape((8, CH),...]
    all_to_all x4 -> x0, waiting for transfers between devices: 55.5 us -> none  [the longest x2 38.4 us: summed_on_arrival(): tiles = lax.all_to_all(in_blocks(array, dim, peers), axis, 0, 0, tiled=True)]
    all_to_all x4 -> x0, starting transfers between devices: 31.6 us -> none  [the longest x2 20.5 us: summed_on_arrival(): tiles = lax.all_to_all(in_blocks(array, dim, peers), axis, 0, 0, tiled=True)]
    dot_general x54 -> x0, matrix products: 21.1 us -> none  [the longest x27 13.9 us: local(): jnp.dot(cot_rows, weights[depth_tap, row_tap, col_tap].T, preferred_eleme...]
    slice x29 -> x0, local copies, waits for them, and re-layouts: 16.8 us -> none  [local(): padded_cot[:, 2 - depth_tap:2 - depth_tap + planes, 2 - row_tap:2 - row_t...]
    ppermute x2 -> x0, starting transfers between devices: 10.1 us -> none  [the longest x1 5.49 us: padded(): after = lax.ppermute(first, axis, down)]
    broadcast_in_dim x2 -> x0, other arithmetic: 6.75 us -> none  [copy_for_each(): copies = jnp.broadcast_to(array, (lax.axis_size(axis), *array.shape))]
    unnamed x61 -> x21, local copies, waits for them, and re-layouts: 4.04 us -> 10 us
  transfers between devices with their start and end apart: 6 -> 0, of which waited for: 5 -> 0; matrix products, arithmetic and copies ran while one was open for 16% -> 0% of each run, Pallas kernels for 0% -> 0%
where the time goes in v1:
time: 76.1 us; the launch traced here: 75.8 us
  Pallas kernels  65 us (85%)
  local copies, waits for them, and re-layouts  10.1 us (13%)
    pallas_call x1, Pallas kernels, step(): pl.pallas_call(kernel, out_shape=(shape((H, W, CH), bf16), shape((8, CH),...  65 us
    unnamed x21, local copies, waits for them, and re-layouts  10 us

profile of v1, /device:TPU:1, one launch (start us, length us, event | category | flops | bytes accessed | tf_op | source)
XLA Modules:
  0.0 75.8 jit_solution(11925665209063876418)
XLA Ops:
  0.6 0.0 copy-start.4
  0.6 0.7 copy-done.4
  1.3 0.0 copy-start.5
  1.3 0.7 copy-done.5
  2.0 0.0 copy-start.6
  2.0 0.7 copy-done.6
  2.7 0.0 copy-start
  2.7 1.2 %copy-done = bf16[3,3,3,128,128]{4,3,2,1,0:T(8,128)(2,1)S(1)} copy-done((bf16[3,3,3,128,128]{4,3,2,1,0:T(8,128)(2,1)S(1)}, bf16[3,3,3,128,128]{4,3,2,1,0:T(8,128)(2,1)}, u32[]{:S(2)}) %copy-start) | copy-done | bytes 884760
  3.9 0.0 copy-start.1
  3.9 0.9 %copy-done.1 = bf16[1,1,64,16,128]{4,3,2,1,0:T(8,128)(2,1)S(1)} copy-done((bf16[1,1,64,16,128]{4,3,2,1,0:T(8,128)(2,1)S(1)}, bf16[1,1,64,16,128]{4,3,2,1,0:T(8,128)(2,1)}, u32[]{:S(2)}) %copy-start.1) | copy-done | bytes 262168
  4.8 0.0 copy-start.2
  4.9 0.9 %copy-done.2 = bf16[1,1,64,16,128]{4,3,2,1,0:T(8,128)(2,1)S(1)} copy-done((bf16[1,1,64,16,128]{4,3,2,1,0:T(8,128)(2,1)S(1)}, bf16[1,1,64,16,128]{4,3,2,1,0:T(8,128)(2,1)}, u32[]{:S(2)}) %copy-start.2) | copy-done | bytes 262168
  5.8 0.0 copy-start.3
  5.8 0.9 %copy-done.3 = bf16[1,1,64,16,128]{4,3,2,1,0:T(8,128)(2,1)S(1)} copy-done((bf16[1,1,64,16,128]{4,3,2,1,0:T(8,128)(2,1)S(1)}, bf16[1,1,64,16,128]{4,3,2,1,0:T(8,128)(2,1)}, u32[]{:S(2)}) %copy-start.3) | copy-done | bytes 262168
  6.8 65.0 %conv_step.1 = (bf16[64,16,128]{2,1,0:T(8,128)(2,1)S(1)}, f32[8,128]{1,0:T(8,128)S(1)}, f32[8,128]{1,0:T(8,128)S(1)}, f32[8,128]{1,0:T(8,128)S(1)}, f32[8,128]{1,0:T(8,128)S(1)}, /*index=5*/bf16[3456,128]{1,0:T(8,128)(2,1)S(1)}) custom-call(bf16[64,16,128]{2,1,0:T(8,128)(2,1)S(1)} %bitcast.21, bf16[64,16,128]{2,1,0:T(8,128)(2,1)S(1)} %bitcast.22, ...), custom_call_target="tpu_custom_call" | custom-call | tf_op jit(solution)/shard_map/conv_step/pallas_call | solution.py:289
  71.8 0.7 copy.22
  72.5 0.6 copy.23
  73.1 0.6 copy.24
  73.7 0.6 copy.25
  74.2 0.6 copy.26
  74.8 0.9 %copy.27 = bf16[3,3,3,128,128]{4,3,2,1,0:T(8,128)(2,1)} copy(bf16[3,3,3,128,128]{4,3,2,1,0:T(8,128)(2,1)S(1)} %bitcast.20) | data formatting | bytes 1769472
  (5 shorter events, 0.0 us)
Async XLA Ops:
  0.6 0.7 copy-start.4
  1.3 0.7 copy-start.5
  2.0 0.7 copy-start.6
  2.7 1.2 %copy-start = (bf16[3,3,3,128,128]{4,3,2,1,0:T(8,128)(2,1)S(1)}, bf16[3,3,3,128,128]{4,3,2,1,0:T(8,128)(2,1)}, u32[]{:S(2)}) copy-start(bf16[3,3,3,128,128]{4,3,2,1,0:T(8,128)(2,1)} %param.10) | copy-start | bytes 2654212
  3.9 0.9 %copy-start.1 = (bf16[1,1,64,16,128]{4,3,2,1,0:T(8,128)(2,1)S(1)}, bf16[1,1,64,16,128]{4,3,2,1,0:T(8,128)(2,1)}, u32[]{:S(2)}) copy-start(bf16[1,1,64,16,128]{4,3,2,1,0:T(8,128)(2,1)} %param.7) | copy-start | bytes 786436
  4.8 0.9 %copy-start.2 = (bf16[1,1,64,16,128]{4,3,2,1,0:T(8,128)(2,1)S(1)}, bf16[1,1,64,16,128]{4,3,2,1,0:T(8,128)(2,1)}, u32[]{:S(2)}) copy-start(bf16[1,1,64,16,128]{4,3,2,1,0:T(8,128)(2,1)} %param.8) | copy-start | bytes 786436
  5.8 0.9 %copy-start.3 = (bf16[1,1,64,16,128]{4,3,2,1,0:T(8,128)(2,1)S(1)}, bf16[1,1,64,16,128]{4,3,2,1,0:T(8,128)(2,1)}, u32[]{:S(2)}) copy-start(bf16[1,1,64,16,128]{4,3,2,1,0:T(8,128)(2,1)} %param.9) | copy-start | bytes 786436

commit v2 on v1

v2 whole, which is shorter than its diff:
```python
import jax
import jax.numpy as jnp
from jax import lax
from jax.experimental import pallas as pl
from jax.experimental.pallas import tpu as pltpu
from jax.sharding import PartitionSpec as P

first_fix = 1.0
second_fix = 0.63230457524

NX, NY, NC, NZ = 4, 8, 2, 8
H, W, CH = 64, 16, 128
POS = H * W
ROWS = 54
PAD = 56
SHARE = 864
COUNT = 8 * 64 * H * W
MESH = pl.DeviceIdType.MESH


def first_row(z):
    return (27 * z) // 4


def kernel(
    act_hbm, pre_hbm, og_hbm, w_hbm, ma_hbm, mo_hbm, se_hbm,
    gi_ref, fg_ref, nm_ref, ns_ref, nma_ref, nw_ref,
    act, pre, og, wts, ma, mo, se, in_sem,
    cc, halo, halo_s, halo_r,
    xs, act_t, flat, give,
    r0, r0_s, r0_r,
    s1, rel, rel_s, rel_r, r1, near_s, near_r, relayed, sum_s, sum_r,
    s2, r2, r2_s, r2_r,
    s3, win, r3, r3_s, r3_r,
    out_win, r4, r4_s, r4_r, block,
    full, y_s, y_r, up_s, up_r, dn_s, dn_r, fw_s, fw_r, c_s, c_r,
):
    p = lax.axis_index("depth")
    z = lax.axis_index("samp")
    n_depth = NX * NY * NC
    c = lax.rem(p, NC)
    y = lax.rem(p // NC, NY)
    x = p // (NC * NY)

    def dev(xx, yy, ccore, zz):
        return {"depth": (xx * NY + yy) * NC + ccore, "samp": zz}

    below = {"depth": lax.rem(p + n_depth - 1, n_depth), "samp": z}
    above = {"depth": lax.rem(p + 1, n_depth), "samp": z}
    partner = dev(x, y, 1 - c, z)
    xk = [lax.rem(x + k, NX) for k in range(NX)]
    x_up = dev(xk[1], y, c, z)
    x_dn = dev(xk[3], y, c, z)
    y_peer = [dev(x, lax.rem(y + k, NY), c, z) for k in range(NY)]
    z_peer = [dev(x, y, c, lax.rem(z + k, NZ)) for k in range(NZ)]

    loads = [
        pltpu.make_async_copy(src, dst, in_sem.at[i])
        for i, (src, dst) in enumerate(
            (
                (pre_hbm, pre),
                (og_hbm, og),
                (act_hbm, act),
                (w_hbm, wts),
                (ma_hbm, ma),
                (mo_hbm, mo),
                (se_hbm, se),
            )
        )
    ]
    for load in loads:
        load.start()

    barrier = pltpu.get_barrier_semaphore()
    peers = [below, above, x_up, x_dn] + y_peer[1:] + z_peer[1:]
    for peer in peers:
        pl.semaphore_signal(barrier, inc=1, device_id=peer, device_id_type=MESH)

    loads[0].wait()
    loads[1].wait()

    @pl.loop(0, 8)
    def _(i):
        part = pl.ds(i * 8, 8)
        slope = jnp.where(pre[part].astype(jnp.float32) > 0, jnp.float32(1.0), jnp.float32(0.01))
        cc[part] = (og[part].astype(jnp.float32) * slope).astype(jnp.bfloat16)

    pl.semaphore_wait(barrier, len(peers))

    started = []

    def remote(src, dst, s, r, to):
        copy = pltpu.make_async_remote_copy(
            src_ref=src, dst_ref=dst, send_sem=s, recv_sem=r, device_id=to, device_id_type=MESH
        )
        copy.start()
        started.append(copy)
        return copy

    from_below = remote(cc, halo.at[0], halo_s.at[0], halo_r.at[0], above)
    from_above = remote(cc, halo.at[1], halo_s.at[1], halo_r.at[1], below)

    def spread(src, plane, keep):
        zero_row = jnp.zeros((W, CH), jnp.bfloat16)
        for col in range(3):
            xs[col, plane, 0] = zero_row
            xs[col, plane, H + 1] = zero_row

        @pl.loop(0, 8)
        def _(i):
            v = src[pl.ds(i * 8, 8)].astype(jnp.float32).reshape(8 * W, CH)
            if keep is not None:
                v = jnp.where(keep, v, 0.0)
            w = lax.broadcasted_iota(jnp.int32, (8 * W, CH), 0) % W
            after = jnp.where(w == W - 1, 0.0, pltpu.roll(v, 8 * W - 1, 0))
            before = jnp.where(w == 0, 0.0, pltpu.roll(v, 1, 0))
            for col, moved in ((0, after), (1, v), (2, before)):
                xs[col, plane, pl.ds(1 + i * 8, 8)] = moved.reshape(8, W, CH).astype(jnp.bfloat16)

    def taps(a):
        @pl.loop(0, 3)
        def _(b):
            right = jnp.concatenate(
                [xs[col, 2 - a, pl.ds(2 - b, H)].reshape(POS, CH) for col in range(3)], axis=1
            )
            raw = jnp.dot(act_t[...], right, preferred_element_type=jnp.float32)
            for col in range(3):
                row = pl.multiple_of(((a * 3 + b) * 3 + col) * CH, CH)
                flat[pl.ds(row, CH)] = raw[:, col * CH : (col + 1) * CH]

    loads[2].wait()
    act_t[...] = act[...].reshape(POS, CH).astype(jnp.float32).T.astype(jnp.bfloat16)
    spread(cc, 1, None)
    taps(1)
    from_below.wait_recv()
    spread(halo.at[0], 0, p > 0)
    taps(2)
    from_above.wait_recv()
    spread(halo.at[1], 2, p < n_depth - 1)
    taps(0)

    core_copies = {}
    for k in (2, 1, 3, 0):
        xx = xk[k]

        @pl.loop(0, NY)
        def _(yy):
            give[xx, yy, 0:ROWS] = flat[pl.ds(((xx * NY + yy) * NC + 1 - c) * ROWS, ROWS)]

        core_copies[k] = remote(give.at[xx], r0.at[xx], r0_s.at[k], r0_r.at[k], partner)

    def both_cores(k):
        xx = xk[k]
        core_copies[k].wait_recv()

        @pl.loop(0, NY)
        def _(yy):
            own = flat[pl.ds(((xx * NY + yy) * NC + c) * ROWS, ROWS)]
            s1[xx, yy, 0:ROWS] = own + r0[xx, yy, 0:ROWS]

    order = (4, 3, 5, 2, 6, 1, 7, 0)
    by_down = {k: i % 2 == 0 for i, k in enumerate(order)}
    yk = [lax.rem(y + k, NY) for k in range(NY)]
    relays, nears, sums = {}, {}, {}
    both_cores(2)
    for k in order:
        to = x_dn if by_down[k] else x_up
        relays[k] = remote(s1.at[xk[2], yk[k]], rel.at[k], rel_s.at[k], rel_r.at[k], to)
    both_cores(1)
    both_cores(3)

    def near(k):
        if by_down[k]:
            nears[k] = remote(s1.at[xk[1], yk[k]], r1.at[0, k], near_s.at[k], near_r.at[k], x_up)
        else:
            nears[k] = remote(s1.at[xk[3], yk[k]], r1.at[1, k], near_s.at[k], near_r.at[k], x_dn)

    near(order[0])
    near(order[1])
    both_cores(0)

    loads[3].wait()

    @pl.loop(0, 4)
    def _(m):
        acc = jnp.zeros((POS // 4, CH), jnp.float32)
        for a in range(3):
            for b in range(3):
                left = jnp.concatenate(
                    [
                        xs[col, 2 - a, pl.ds(2 - b + m * (H // 4), H // 4)].reshape(POS // 4, CH)
                        for col in range(3)
                    ],
                    axis=1,
                )
                right = jnp.concatenate([wts[(a * 3 + b) * 3 + col] for col in range(3)], axis=1)
                acc = acc + lax.dot_general(
                    left, right, (((1,), (1,)), ((), ())), preferred_element_type=jnp.float32
                )
        gi_ref[pl.ds(m * (H // 4), H // 4)] = acc.reshape(H // 4, W, CH).astype(jnp.bfloat16)

    y_copies = {}

    def root(k):
        nears[k].wait_recv()
        sums[k].wait_recv()
        s2[k] = s1[x, yk[k]] + r1[0, k] + r1[1, k]
        if k:
            y_copies[k] = remote(
                s2.at[k], r2.at[k - 1], r2_s.at[k - 1], r2_r.at[k - 1], y_peer[k]
            )

    for i, k in enumerate(order):
        if i + 2 < NY:
            near(order[i + 2])
        relays[k].wait_recv()
        if by_down[k]:
            relayed[k] = s1[xk[3], yk[k]] + rel[k]
            sums[k] = remote(relayed.at[k], r1.at[1, k], sum_s.at[k], sum_r.at[k], x_dn)
        else:
            relayed[k] = s1[xk[1], yk[k]] + rel[k]
            sums[k] = remote(relayed.at[k], r1.at[0, k], sum_s.at[k], sum_r.at[k], x_up)
        if i >= 3:
            root(order[i - 3])
    for k in order[-3:]:
        root(k)

    total = s2[0]
    for k in (7, 1, 6, 2, 5, 3, 4):
        y_copies[k].wait_recv()
        total = total + r2[k - 1]
    s3[...] = total

    for zz in range(NZ):
        win[zz] = s3[first_row(zz) : first_row(zz) + 8]
    far_first = (4, 3, 5, 2, 6, 1, 7)
    z_copies = [
        remote(win.at[lax.rem(z + k, NZ)], r3.at[k - 1], r3_s.at[k - 1], r3_r.at[k - 1], z_peer[k])
        for k in far_first
    ]
    for copy in z_copies:
        copy.wait_recv()
    raw = win[z]
    for k in range(1, NZ):
        raw = raw + r3[k - 1]

    for load in loads[4:]:
        load.wait()
    off = lax.rem(96 * z, 128)
    lane = lax.broadcasted_iota(jnp.int32, (8, CH), 1)
    row = lax.broadcasted_iota(jnp.int32, (8, CH), 0)
    turned = pltpu.roll(raw, lax.rem(128 - off, 128), 1)
    raw = jnp.where(lane < 128 - off, turned, pltpu.roll(turned, 7, 0))
    filter_grad = raw * jnp.float32(1.0 / COUNT**0.5)

    def wide(ref):
        return jnp.concatenate([ref[...], jnp.zeros((8 * CH - SHARE,), jnp.float32)]).reshape(8, CH)

    new_moment = 0.9 * wide(mo) + 0.1 * filter_grad
    new_second = 0.999 * wide(se) + 0.001 * filter_grad * filter_grad
    new_master = wide(ma) - 0.01 * (new_moment / first_fix) / (
        jnp.sqrt(new_second / second_fix) + 1e-08
    )

    turned = pltpu.roll(new_master, off, 1)
    moved = jnp.where(lane >= off, turned, pltpu.roll(turned, 1, 0))
    place = row * CH + lane
    mine = jnp.where((place >= off) & (place < off + SHARE), moved, 0.0)
    out_win[...] = mine
    r4[z] = mine
    share_copies = [
        remote(out_win, r4.at[z], r4_s.at[k - 1], r4_r.at[k - 1], z_peer[k]) for k in far_first
    ]
    fg_ref[...] = filter_grad
    nm_ref[...] = new_moment
    ns_ref[...] = new_second
    nma_ref[...] = new_master
    block[...] = jnp.zeros_like(block)
    for copy in share_copies:
        copy.wait_recv()
    for zz in range(NZ):
        part = pl.ds(first_row(zz), 8)
        block[part] = block[part] + r4[zz]
    full[c, x, y] = block[0:PAD].astype(jnp.bfloat16)

    gather_y = {}
    for k in far_first:
        gather_y[k] = remote(
            full.at[c, x, y], full.at[c, x, y], y_s.at[k - 1], y_r.at[k - 1], y_peer[k]
        )
    near_first = (0, 1, 7, 2, 6, 3, 5, 4)
    up, down, onward, gather_c = {}, {}, {}, {}

    def to_partner(k):
        part = full.at[c, xk[k]]
        gather_c[k] = remote(part, part, c_s.at[k], c_r.at[k], partner)

    src_y = [lax.rem(y + NY - k, NY) for k in range(NY)]
    for k in near_first:
        if k:
            gather_y[k].wait_recv()
        part = full.at[c, x, src_y[k]]
        up[k] = remote(part, part, up_s.at[k], up_r.at[k], x_up)
        down[k] = remote(part, part, dn_s.at[k], dn_r.at[k], x_dn)
    to_partner(0)
    for i, k in enumerate(near_first):
        up[k].wait_recv()
        down[k].wait_recv()
        if i % 2 == 0:
            part = full.at[c, xk[3], src_y[k]]
            onward[k] = remote(part, part, fw_s.at[k], fw_r.at[k], x_up)
        else:
            part = full.at[c, xk[1], src_y[k]]
            onward[k] = remote(part, part, fw_s.at[k], fw_r.at[k], x_dn)
    to_partner(3)
    to_partner(1)

    def lay_out(k):
        xx = xk[k]
        gather_c[k].wait_recv()
        for yy in range(NY):
            for cr in range(NC):
                start = (yy * NC + cr) * ROWS
                nw_ref[xx, start : start + ROWS] = full[cr, xx, yy, 0:ROWS]

    lay_out(0)
    lay_out(3)
    lay_out(1)
    for k in near_first:
        onward[k].wait_recv()
    to_partner(2)
    lay_out(2)

    for copy in started:
        copy.wait_send()


def write_kernel(gi, fg, nm, ns, nma, nw, gi_o, fg_o, nm_o, ns_o, nma_o, nw_o, sem):
    copies = [
        pltpu.make_async_copy(src, dst, sem.at[i])
        for i, (src, dst) in enumerate(
            ((nw, nw_o), (gi, gi_o), (fg, fg_o), (nm, nm_o), (ns, ns_o), (nma, nma_o))
        )
    ]
    for copy in copies:
        copy.start()
    for copy in copies:
        copy.wait()


def step(*operands):
    vmem = pl.BlockSpec(memory_space=pltpu.VMEM)
    hbm = pl.BlockSpec(memory_space=pltpu.HBM)
    f32, bf16 = jnp.float32, jnp.bfloat16
    shape = jax.ShapeDtypeStruct

    def dma(n):
        return pltpu.SemaphoreType.DMA((n,))

    plane = pltpu.VMEM((H, W, CH), bf16)
    return pl.pallas_call(
        kernel,
        out_shape=(
            shape((H, W, CH), bf16),
            shape((8, CH), f32),
            shape((8, CH), f32),
            shape((8, CH), f32),
            shape((8, CH), f32),
            shape((NX, NY * NC * ROWS, CH), bf16),
        ),
        in_specs=[hbm] * 7,
        out_specs=(vmem,) * 6,
        scratch_shapes=[
            plane,
            plane,
            plane,
            pltpu.VMEM((27, CH, CH), bf16),
            pltpu.VMEM((SHARE,), f32),
            pltpu.VMEM((SHARE,), f32),
            pltpu.VMEM((SHARE,), f32),
            dma(7),
            plane,
            pltpu.VMEM((2, H, W, CH), bf16),
            dma(2),
            dma(2),
            pltpu.VMEM((3, 3, H + 2, W, CH), bf16),
            pltpu.VMEM((CH, POS), bf16),
            pltpu.VMEM((NX * NY * NC * ROWS, CH), f32),
            pltpu.VMEM((NX, NY, PAD, CH), f32),
            pltpu.VMEM((NX, NY, PAD, CH), f32),
            dma(NX),
            dma(NX),
            pltpu.VMEM((NX, NY, PAD, CH), f32),
            pltpu.VMEM((NY, PAD, CH), f32),
            dma(NY),
            dma(NY),
            pltpu.VMEM((2, NY, PAD, CH), f32),
            dma(NY),
            dma(NY),
            pltpu.VMEM((NY, PAD, CH), f32),
            dma(NY),
            dma(NY),
            pltpu.VMEM((NY, PAD, CH), f32),
            pltpu.VMEM((NY - 1, PAD, CH), f32),
            dma(NY - 1),
            dma(NY - 1),
            pltpu.VMEM((PAD, CH), f32),
            pltpu.VMEM((NZ, 8, CH), f32),
            pltpu.VMEM((NZ - 1, 8, CH), f32),
            dma(NZ - 1),
            dma(NZ - 1),
            pltpu.VMEM((8, CH), f32),
            pltpu.VMEM((NZ, 8, CH), f32),
            dma(NZ - 1),
            dma(NZ - 1),
            pltpu.VMEM((64, CH), f32),
            pltpu.VMEM((NC, NX, NY, PAD, CH), bf16),
            dma(NY - 1),
            dma(NY - 1),
            dma(NY),
            dma(NY),
            dma(NY),
            dma(NY),
            dma(NY),
            dma(NY),
            dma(NX),
            dma(NX),
        ],
        compiler_params=pltpu.CompilerParams(
            collective_id=0, has_side_effects=True, vmem_limit_bytes=40 * 1024 * 1024
        ),
        name="conv_step",
    )(*[pltpu.with_memory_space_constraint(a, pltpu.HBM) for a in operands])


def write(*results):
    return pl.pallas_call(
        write_kernel,
        out_shape=tuple(jax.ShapeDtypeStruct(a.shape, a.dtype) for a in results),
        in_specs=[pl.BlockSpec(memory_space=pltpu.VMEM)] * 6,
        out_specs=(pl.BlockSpec(memory_space=pltpu.HBM),) * 6,
        scratch_shapes=[pltpu.SemaphoreType.DMA((6,))],
        compiler_params=pltpu.CompilerParams(vmem_limit_bytes=4 * 1024 * 1024),
        name="write_out",
    )(*results)


def local(activations, preact, out_grad, weights, master, moment, second):
    plane = (H, W, CH)
    opt = [master, moment, second]
    gi, fg, nm, ns, nma, nw = write(
        *step(
            activations.reshape(plane),
            preact.reshape(plane),
            out_grad.reshape(plane),
            weights.reshape(27, CH, CH),
            *opt,
        )
    )
    own = [a.reshape(-1)[:SHARE] for a in (fg, nm, ns, nma)]
    return (gi.reshape(activations.shape), *own, nw.reshape(weights.shape))


def solution(mesh):
    volume = P("samp", "depth", None, None, None)
    shares = P(("depth", "samp"))
    return jax.shard_map(
        local,
        mesh=mesh,
        in_specs=(volume, volume, volume, P(), shares, shares, shares),
        out_specs=(volume, shares, shares, shares, shares, P()),
        check_vma=False,
    )
```

time: 76.1 us -> 63.5 us (0.83)
  local copies, waits for them, and re-layouts: 10.1 us -> 0 us
  Pallas kernels: 65 us -> 62.7 us
    unnamed x21 -> x0, local copies, waits for them, and re-layouts: 10 us -> none
    pallas_call x1, Pallas kernels: 65 us -> 61.6 us  [step(): pl.pallas_call(kernel, out_shape=(shape((H, W, CH), bf16), shape((8, CH),...]
    pallas_call x0 -> x1, Pallas kernels: none -> 1.06 us  [write(): pl.pallas_call(write_kernel, out_shape=tuple((jax.ShapeDtypeStruct(a.shap...]
where the time goes in v2:
time: 63.5 us; the launch traced here: 63.3 us
  Pallas kernels  62.7 us (99%)
  between operations  0.64 us (1%)
    pallas_call x1, Pallas kernels, step(): pl.pallas_call(kernel, out_shape=(shape((H, W, CH), bf16), shape((8, CH),...  61.6 us

profile of v2, /device:TPU:1, one launch (start us, length us, event | category | flops | bytes accessed | tf_op | source)
XLA Modules:
  0.0 63.3 jit_solution(24621155673494129)
XLA Ops:
  0.6 61.6 %conv_step.1 = (bf16[64,16,128]{2,1,0:T(8,128)(2,1)S(1)}, f32[8,128]{1,0:T(8,128)S(1)}, f32[8,128]{1,0:T(8,128)S(1)}, f32[8,128]{1,0:T(8,128)S(1)}, f32[8,128]{1...) custom-call(bf16[64,16,128]{2,1,0:T(8,128)(2,1)} %bitcast.15, bf16[64,16,128]{2,1,0:T(8,128)(2,1)} %bitcast.16, ...), custom_call_target="tpu_custom_call" | custom-call | tf_op jit(solution)/shard_map/conv_step/pallas_call | solution.py:361
  62.3 1.1 %write_out.1 = (bf16[64,16,128]{2,1,0:T(8,128)(2,1)}, f32[8,128]{1,0:T(8,128)}, f32[8,128]{1,0:T(8,128)}, f32[8,128]{1,0:T(8,128)}, f32[8,128]{1,0:T(8,128)}, /*index=5*/bf16[4,864,128]{2,1,0:T(8,128)(2,1)}) custom-call(bf16[64,16,128]{2,1,0:T(8,128)(2,1)S(1)} %get-tuple-element.18.gi, f32[8,128]{1,0:T(8,128)S(1)} %get-tuple-element.19.fg, ...), custom_call_target="tpu_custom_call" | custom-call | tf_op jit(solution)/shard_map/write_out/pallas_call | solution.py:437

commit v3 on v2

--- a/solution.py
+++ b/solution.py
@@ -26,7 +26,7 @@
     act_hbm, pre_hbm, og_hbm, w_hbm, ma_hbm, mo_hbm, se_hbm,
     gi_ref, fg_ref, nm_ref, ns_ref, nma_ref, nw_ref,
     act, pre, og, wts, ma, mo, se, in_sem,
-    cc, halo, halo_s, halo_r,
+    cc, halo, halo_s, halo_r, known,
     xs, act_t, flat, give,
     r0, r0_s, r0_r,
     s1, rel, rel_s, rel_r, r1, near_s, near_r, relayed, sum_s, sum_r,
@@ -45,11 +45,11 @@
     def dev(xx, yy, ccore, zz):
         return {"depth": (xx * NY + yy) * NC + ccore, "samp": zz}
 
-    below = {"depth": lax.rem(p + n_depth - 1, n_depth), "samp": z}
-    above = {"depth": lax.rem(p + 1, n_depth), "samp": z}
     partner = dev(x, y, 1 - c, z)
+    other = {"depth": lax.rem(p + n_depth + 2 * c - 1, n_depth), "samp": z}
     xk = [lax.rem(x + k, NX) for k in range(NX)]
     x_up = dev(xk[1], y, c, z)
+    x_far = dev(xk[2], y, c, z)
     x_dn = dev(xk[3], y, c, z)
     y_peer = [dev(x, lax.rem(y + k, NY), c, z) for k in range(NY)]
     z_peer = [dev(x, y, c, lax.rem(z + k, NZ)) for k in range(NZ)]
@@ -72,7 +72,7 @@
         load.start()
 
     barrier = pltpu.get_barrier_semaphore()
-    peers = [below, above, x_up, x_dn] + y_peer[1:] + z_peer[1:]
+    peers = [partner, other, x_up, x_dn, y_peer[1], y_peer[7], z_peer[1], z_peer[7]]
     for peer in peers:
         pl.semaphore_signal(barrier, inc=1, device_id=peer, device_id_type=MESH)
 
@@ -86,6 +86,18 @@
         cc[part] = (og[part].astype(jnp.float32) * slope).astype(jnp.bfloat16)
 
     pl.semaphore_wait(barrier, len(peers))
+
+    flows = ((y_peer[1], 3), (y_peer[7], 4), (z_peer[1], 3), (z_peer[7], 4), (x_up, 2))
+
+    def pass_on(hops):
+        for i, (_, last) in enumerate(flows):
+            if 2 < hops <= last + 1:
+                pl.semaphore_wait(known.at[i, hops - 3], 1)
+        for i, (to, last) in enumerate(flows):
+            if hops <= last:
+                pl.semaphore_signal(
+                    known.at[i, hops - 2], inc=1, device_id=to, device_id_type=MESH
+                )
 
     started = []
 
@@ -97,8 +109,9 @@
         started.append(copy)
         return copy
 
-    from_below = remote(cc, halo.at[0], halo_s.at[0], halo_r.at[0], above)
-    from_above = remote(cc, halo.at[1], halo_s.at[1], halo_r.at[1], below)
+    from_partner = remote(cc, halo.at[0], halo_s.at[0], halo_r.at[0], partner)
+    from_other = remote(cc, halo.at[1], halo_s.at[1], halo_r.at[1], other)
+    pass_on(2)
 
     def spread(src, plane, keep):
         zero_row = jnp.zeros((W, CH), jnp.bfloat16)
@@ -132,12 +145,15 @@
     act_t[...] = act[...].reshape(POS, CH).astype(jnp.float32).T.astype(jnp.bfloat16)
     spread(cc, 1, None)
     taps(1)
-    from_below.wait_recv()
-    spread(halo.at[0], 0, p > 0)
-    taps(2)
-    from_above.wait_recv()
-    spread(halo.at[1], 2, p < n_depth - 1)
-    taps(0)
+    pass_on(3)
+    from_partner.wait_recv()
+    spread(halo.at[0], 2 * (1 - c), None)
+    taps(2 * c)
+    pass_on(4)
+    from_other.wait_recv()
+    spread(halo.at[1], 2 * c, jnp.where(c == 0, p > 0, p < n_depth - 1))
+    taps(2 - 2 * c)
+    pass_on(5)
 
     core_copies = {}
     for k in (2, 1, 3, 0):
@@ -302,10 +318,14 @@
         part = full.at[c, x, src_y[k]]
         up[k] = remote(part, part, up_s.at[k], up_r.at[k], x_up)
         down[k] = remote(part, part, dn_s.at[k], dn_r.at[k], x_dn)
+        if k in (3, 5, 4):
+            onward[k] = remote(part, part, fw_s.at[k], fw_r.at[k], x_far)
     to_partner(0)
     for i, k in enumerate(near_first):
         up[k].wait_recv()
         down[k].wait_recv()
+        if k in onward:
+            continue
         if i % 2 == 0:
             part = full.at[c, xk[3], src_y[k]]
             onward[k] = remote(part, part, fw_s.at[k], fw_r.at[k], x_up)
@@ -383,6 +403,7 @@
             pltpu.VMEM((2, H, W, CH), bf16),
             dma(2),
             dma(2),
+            pltpu.SemaphoreType.REGULAR((5, 3)),
             pltpu.VMEM((3, 3, H + 2, W, CH), bf16),
             pltpu.VMEM((CH, POS), bf16),
             pltpu.VMEM((NX * NY * NC * ROWS, CH), f32),

time: 63.5 us -> 60.9 us (0.959)
  Pallas kernels: 62.7 us -> 60.1 us
    pallas_call x1, Pallas kernels: 61.6 us -> 59.1 us  [step(): pl.pallas_call(kernel, out_shape=(shape((H, W, CH), bf16), shape((8, CH),...]
where the time goes in v3:
time: 60.9 us; the launch traced here: 60.8 us
  Pallas kernels  60.1 us (99%)
  between operations  0.64 us (1%)
    pallas_call x1, Pallas kernels, step(): pl.pallas_call(kernel, out_shape=(shape((H, W, CH), bf16), shape((8, CH),...  59.1 us

profile of v3, /device:TPU:1, one launch (start us, length us, event | category | flops | bytes accessed | tf_op | source)
XLA Modules:
  0.0 60.8 jit_solution(7177072194843988599)
XLA Ops:
  0.6 59.1 %conv_step.1 = (bf16[64,16,128]{2,1,0:T(8,128)(2,1)S(1)}, f32[8,128]{1,0:T(8,128)S(1)}, f32[8,128]{1,0:T(8,128)S(1)}, f32[8,128]{1,0:T(8,128)S(1)}, f32[8,128]{1...) custom-call(bf16[64,16,128]{2,1,0:T(8,128)(2,1)} %bitcast.15, bf16[64,16,128]{2,1,0:T(8,128)(2,1)} %bitcast.16, ...), custom_call_target="tpu_custom_call" | custom-call | tf_op jit(solution)/shard_map/conv_step/pallas_call | solution.py:381
  59.7 1.1 %write_out.1 = (bf16[64,16,128]{2,1,0:T(8,128)(2,1)}, f32[8,128]{1,0:T(8,128)}, f32[8,128]{1,0:T(8,128)}, f32[8,128]{1,0:T(8,128)}, f32[8,128]{1,0:T(8,128)}, /*index=5*/bf16[4,864,128]{2,1,0:T(8,128)(2,1)}) custom-call(bf16[64,16,128]{2,1,0:T(8,128)(2,1)S(1)} %get-tuple-element.18.gi, f32[8,128]{1,0:T(8,128)S(1)} %get-tuple-element.19.fg, ...), custom_call_target="tpu_custom_call" | custom-call | tf_op jit(solution)/shard_map/write_out/pallas_call | solution.py:458

commit v4 on v3

--- a/solution.py
+++ b/solution.py
@@ -29,7 +29,7 @@
     cc, halo, halo_s, halo_r, known,
     xs, act_t, flat, give,
     r0, r0_s, r0_r,
-    s1, rel, rel_s, rel_r, r1, near_s, near_r, relayed, sum_s, sum_r,
+    s1, r1, x1_s, x1_r,
     s2, r2, r2_s, r2_r,
     s3, win, r3, r3_s, r3_r,
     out_win, r4, r4_s, r4_r, block,
@@ -141,59 +141,59 @@
                 row = pl.multiple_of(((a * 3 + b) * 3 + col) * CH, CH)
                 flat[pl.ds(row, CH)] = raw[:, col * CH : (col + 1) * CH]
 
+    def exchange(group, first, count):
+        @pl.loop(0, count)
+        def _(j):
+            q = first + j
+            give[q, 0:ROWS] = flat[pl.ds((q * NC + 1 - c) * ROWS, ROWS)]
+
+        part = pl.ds(first, count)
+        return remote(give.at[part], r0.at[part], r0_s.at[group], r0_r.at[group], partner)
+
+    def both_cores(first, count):
+        @pl.loop(0, count)
+        def _(j):
+            q = first + j
+            own = flat[pl.ds((q * NC + c) * ROWS, ROWS)]
+            s1[q, 0:ROWS] = own + r0[q, 0:ROWS]
+
     loads[2].wait()
     act_t[...] = act[...].reshape(POS, CH).astype(jnp.float32).T.astype(jnp.bfloat16)
     spread(cc, 1, None)
     taps(1)
+    middle = exchange(0, 11, 10)
     pass_on(3)
     from_partner.wait_recv()
     spread(halo.at[0], 2 * (1 - c), None)
     taps(2 * c)
+    early = exchange(1, 21 * c, 11)
+    middle.wait_recv()
+    both_cores(11, 10)
     pass_on(4)
     from_other.wait_recv()
     spread(halo.at[1], 2 * c, jnp.where(c == 0, p > 0, p < n_depth - 1))
     taps(2 - 2 * c)
+    late = exchange(2, 21 * (1 - c), 11)
+    early.wait_recv()
+    both_cores(21 * (1 - c), 11)
     pass_on(5)
-
-    core_copies = {}
-    for k in (2, 1, 3, 0):
-        xx = xk[k]
-
-        @pl.loop(0, NY)
-        def _(yy):
-            give[xx, yy, 0:ROWS] = flat[pl.ds(((xx * NY + yy) * NC + 1 - c) * ROWS, ROWS)]
-
-        core_copies[k] = remote(give.at[xx], r0.at[xx], r0_s.at[k], r0_r.at[k], partner)
-
-    def both_cores(k):
-        xx = xk[k]
-        core_copies[k].wait_recv()
-
-        @pl.loop(0, NY)
-        def _(yy):
-            own = flat[pl.ds(((xx * NY + yy) * NC + c) * ROWS, ROWS)]
-            s1[xx, yy, 0:ROWS] = own + r0[xx, yy, 0:ROWS]
+    late.wait_recv()
+    both_cores(21 * c, 11)
 
     order = (4, 3, 5, 2, 6, 1, 7, 0)
-    by_down = {k: i % 2 == 0 for i, k in enumerate(order)}
     yk = [lax.rem(y + k, NY) for k in range(NY)]
-    relays, nears, sums = {}, {}, {}
-    both_cores(2)
+    x_copies = {}
     for k in order:
-        to = x_dn if by_down[k] else x_up
-        relays[k] = remote(s1.at[xk[2], yk[k]], rel.at[k], rel_s.at[k], rel_r.at[k], to)
-    both_cores(1)
-    both_cores(3)
-
-    def near(k):
-        if by_down[k]:
-            nears[k] = remote(s1.at[xk[1], yk[k]], r1.at[0, k], near_s.at[k], near_r.at[k], x_up)
-        else:
-            nears[k] = remote(s1.at[xk[3], yk[k]], r1.at[1, k], near_s.at[k], near_r.at[k], x_dn)
-
-    near(order[0])
-    near(order[1])
-    both_cores(0)
+        x_copies[k] = [
+            remote(
+                s1.at[xk[j] * NY + yk[k]],
+                r1.at[j - 1, k],
+                x1_s.at[j - 1, k],
+                x1_r.at[j - 1, k],
+                to,
+            )
+            for j, to in ((2, x_far), (1, x_up), (3, x_dn))
+        ]
 
     loads[3].wait()
 
@@ -217,29 +217,14 @@
 
     y_copies = {}
 
-    def root(k):
-        nears[k].wait_recv()
-        sums[k].wait_recv()
-        s2[k] = s1[x, yk[k]] + r1[0, k] + r1[1, k]
+    for k in order:
+        for copy in x_copies[k]:
+            copy.wait_recv()
+        s2[k] = s1[x * NY + yk[k]] + r1[0, k] + r1[1, k] + r1[2, k]
         if k:
             y_copies[k] = remote(
                 s2.at[k], r2.at[k - 1], r2_s.at[k - 1], r2_r.at[k - 1], y_peer[k]
             )
-
-    for i, k in enumerate(order):
-        if i + 2 < NY:
-            near(order[i + 2])
-        relays[k].wait_recv()
-        if by_down[k]:
-            relayed[k] = s1[xk[3], yk[k]] + rel[k]
-            sums[k] = remote(relayed.at[k], r1.at[1, k], sum_s.at[k], sum_r.at[k], x_dn)
-        else:
-            relayed[k] = s1[xk[1], yk[k]] + rel[k]
-            sums[k] = remote(relayed.at[k], r1.at[0, k], sum_s.at[k], sum_r.at[k], x_up)
-        if i >= 3:
-            root(order[i - 3])
-    for k in order[-3:]:
-        root(k)
 
     total = s2[0]
     for k in (7, 1, 6, 2, 5, 3, 4):
@@ -282,6 +267,7 @@
     moved = jnp.where(lane >= off, turned, pltpu.roll(turned, 1, 0))
     place = row * CH + lane
     mine = jnp.where((place >= off) & (place < off + SHARE), moved, 0.0)
+    mine = mine.astype(jnp.bfloat16)
     out_win[...] = mine
     r4[z] = mine
     share_copies = [
@@ -296,7 +282,7 @@
         copy.wait_recv()
     for zz in range(NZ):
         part = pl.ds(first_row(zz), 8)
-        block[part] = block[part] + r4[zz]
+        block[part] = block[part] + r4[zz].astype(jnp.float32)
     full[c, x, y] = block[0:PAD].astype(jnp.bfloat16)
 
     gather_y = {}
@@ -318,20 +304,11 @@
         part = full.at[c, x, src_y[k]]
         up[k] = remote(part, part, up_s.at[k], up_r.at[k], x_up)
         down[k] = remote(part, part, dn_s.at[k], dn_r.at[k], x_dn)
-        if k in (3, 5, 4):
-            onward[k] = remote(part, part, fw_s.at[k], fw_r.at[k], x_far)
+        onward[k] = remote(part, part, fw_s.at[k], fw_r.at[k], x_far)
     to_partner(0)
-    for i, k in enumerate(near_first):
+    for k in near_first:
         up[k].wait_recv()
         down[k].wait_recv()
-        if k in onward:
-            continue
-        if i % 2 == 0:
-            part = full.at[c, xk[3], src_y[k]]
-            onward[k] = remote(part, part, fw_s.at[k], fw_r.at[k], x_up)
-        else:
-            part = full.at[c, xk[1], src_y[k]]
-            onward[k] = remote(part, part, fw_s.at[k], fw_r.at[k], x_dn)
     to_partner(3)
     to_partner(1)
 
@@ -407,20 +384,14 @@
             pltpu.VMEM((3, 3, H + 2, W, CH), bf16),
             pltpu.VMEM((CH, POS), bf16),
             pltpu.VMEM((NX * NY * NC * ROWS, CH), f32),
-            pltpu.VMEM((NX, NY, PAD, CH), f32),
-            pltpu.VMEM((NX, NY, PAD, CH), f32),
-            dma(NX),
-            dma(NX),
-            pltpu.VMEM((NX, NY, PAD, CH), f32),
-            pltpu.VMEM((NY, PAD, CH), f32),
-            dma(NY),
-            dma(NY),
-            pltpu.VMEM((2, NY, PAD, CH), f32),
-            dma(NY),
-            dma(NY),
-            pltpu.VMEM((NY, PAD, CH), f32),
-            dma(NY),
-            dma(NY),
+            pltpu.VMEM((NX * NY, PAD, CH), f32),
+            pltpu.VMEM((NX * NY, PAD, CH), f32),
+            dma(3),
+            dma(3),
+            pltpu.VMEM((NX * NY, PAD, CH), f32),
+            pltpu.VMEM((NX - 1, NY, PAD, CH), f32),
+            pltpu.SemaphoreType.DMA((NX - 1, NY)),
+            pltpu.SemaphoreType.DMA((NX - 1, NY)),
             pltpu.VMEM((NY, PAD, CH), f32),
             pltpu.VMEM((NY - 1, PAD, CH), f32),
             dma(NY - 1),
@@ -430,8 +401,8 @@
             pltpu.VMEM((NZ - 1, 8, CH), f32),
             dma(NZ - 1),
             dma(NZ - 1),
-            pltpu.VMEM((8, CH), f32),
-            pltpu.VMEM((NZ, 8, CH), f32),
+            pltpu.VMEM((8, CH), bf16),
+            pltpu.VMEM((NZ, 8, CH), bf16),
             dma(NZ - 1),
             dma(NZ - 1),
             pltpu.VMEM((64, CH), f32),

time: 60.9 us -> 59.5 us (0.977)
  Pallas kernels: 60.1 us -> 58.8 us
    pallas_call x1, Pallas kernels: 59.1 us -> 57.7 us  [step(): pl.pallas_call(kernel, out_shape=(shape((H, W, CH), bf16), shape((8, CH),...]
where the time goes in v4:
time: 59.5 us; the launch traced here: 59.4 us
  Pallas kernels  58.8 us (99%)
  between operations  0.64 us (1%)
    pallas_call x1, Pallas kernels, step(): pl.pallas_call(kernel, out_shape=(shape((H, W, CH), bf16), shape((8, CH),...  57.7 us

profile of v4, /device:TPU:1, one launch (start us, length us, event | category | flops | bytes accessed | tf_op | source)
XLA Modules:
  0.0 59.4 jit_solution(3082027925573786702)
XLA Ops:
  0.6 57.7 %conv_step.1 = (bf16[64,16,128]{2,1,0:T(8,128)(2,1)S(1)}, f32[8,128]{1,0:T(8,128)S(1)}, f32[8,128]{1,0:T(8,128)S(1)}, f32[8,128]{1,0:T(8,128)S(1)}, f32[8,128]{1...) custom-call(bf16[64,16,128]{2,1,0:T(8,128)(2,1)} %bitcast.15, bf16[64,16,128]{2,1,0:T(8,128)(2,1)} %bitcast.16, ...), custom_call_target="tpu_custom_call" | custom-call | tf_op jit(solution)/shard_map/conv_step/pallas_call | solution.py:358
  58.3 1.1 %write_out.1 = (bf16[64,16,128]{2,1,0:T(8,128)(2,1)}, f32[8,128]{1,0:T(8,128)}, f32[8,128]{1,0:T(8,128)}, f32[8,128]{1,0:T(8,128)}, f32[8,128]{1,0:T(8,128)}, /*index=5*/bf16[4,864,128]{2,1,0:T(8,128)(2,1)}) custom-call(bf16[64,16,128]{2,1,0:T(8,128)(2,1)S(1)} %get-tuple-element.18.gi, f32[8,128]{1,0:T(8,128)S(1)} %get-tuple-element.19.fg, ...), custom_call_target="tpu_custom_call" | custom-call | tf_op jit(solution)/shard_map/write_out/pallas_call | solution.py:429

commit v5 on v4

--- a/solution.py
+++ b/solution.py
@@ -302,15 +302,19 @@
         if k:
             gather_y[k].wait_recv()
         part = full.at[c, x, src_y[k]]
+        onward[k] = remote(part, part, fw_s.at[k], fw_r.at[k], x_far)
         up[k] = remote(part, part, up_s.at[k], up_r.at[k], x_up)
         down[k] = remote(part, part, dn_s.at[k], dn_r.at[k], x_dn)
-        onward[k] = remote(part, part, fw_s.at[k], fw_r.at[k], x_far)
     to_partner(0)
     for k in near_first:
         up[k].wait_recv()
+    to_partner(3)
+    for k in near_first:
         down[k].wait_recv()
-    to_partner(3)
     to_partner(1)
+    for k in near_first:
+        onward[k].wait_recv()
+    to_partner(2)
 
     def lay_out(k):
         xx = xk[k]
@@ -323,9 +327,6 @@
     lay_out(0)
     lay_out(3)
     lay_out(1)
-    for k in near_first:
-        onward[k].wait_recv()
-    to_partner(2)
     lay_out(2)
 
     for copy in started:

time: 59.5 us -> 59.3 us (level)
  no operation moved by 1% of the time
where the time goes in v5:
time: 59.3 us; the launch traced here: 59.1 us
  Pallas kernels  58.5 us (99%)
  between operations  0.64 us (1%)
    pallas_call x1, Pallas kernels, step(): pl.pallas_call(kernel, out_shape=(shape((H, W, CH), bf16), shape((8, CH),...  57.4 us

profile of v5, /device:TPU:1, one launch (start us, length us, event | category | flops | bytes accessed | tf_op | source)
XLA Modules:
  0.0 59.1 jit_solution(6551855805110962659)
XLA Ops:
  0.6 57.4 %conv_step.1 = (bf16[64,16,128]{2,1,0:T(8,128)(2,1)S(1)}, f32[8,128]{1,0:T(8,128)S(1)}, f32[8,128]{1,0:T(8,128)S(1)}, f32[8,128]{1,0:T(8,128)S(1)}, f32[8,128]{1...) custom-call(bf16[64,16,128]{2,1,0:T(8,128)(2,1)} %bitcast.15, bf16[64,16,128]{2,1,0:T(8,128)(2,1)} %bitcast.16, ...), custom_call_target="tpu_custom_call" | custom-call | tf_op jit(solution)/shard_map/conv_step/pallas_call | solution.py:359
  58.1 1.1 %write_out.1 = (bf16[64,16,128]{2,1,0:T(8,128)(2,1)}, f32[8,128]{1,0:T(8,128)}, f32[8,128]{1,0:T(8,128)}, f32[8,128]{1,0:T(8,128)}, f32[8,128]{1,0:T(8,128)}, /*index=5*/bf16[4,864,128]{2,1,0:T(8,128)(2,1)}) custom-call(bf16[64,16,128]{2,1,0:T(8,128)(2,1)S(1)} %get-tuple-element.18.gi, f32[8,128]{1,0:T(8,128)S(1)} %get-tuple-element.19.fg, ...), custom_call_target="tpu_custom_call" | custom-call | tf_op jit(solution)/shard_map/write_out/pallas_call | solution.py:430
